TPU v7x, 32 devices: a whole 2x2x4 slice. The times are simulated.
32 devices in a mesh: blk: 32 (over z, y, x, core).
Axes of the slice: x: 2, y: 2, z: 4, core: 2. Of those that a mesh axis runs over, the one named last changes fastest.
Arguments:
- tensor_blocks: bfloat16 [352, 32, 32, 1024], P('blk')
- block_index: int32 [352, 4], P('blk'), may hold values from 0 to 8, as said below
- starts: float32 [256, 32], P(None, 'blk'), may hold values from -6 to 6
- shifts: float32 [32], replicated, may hold values from 0.5 to 2
Outputs:
- iterate: float32 [256, 32], P(None, 'blk')
- estimate: float32 [32], P('blk')
Inputs may be any that keep to these rules, and one draw needn't show every extreme that they name: `block_index`: every sorted quadruple i <= j <= k <= l of 0 to 7 is held by exactly one slot; every other slot holds 8 in all four entries and is not used. A live slot's block is unchanged when two of its axes with equal block indices are swapped.
All inputs are finite; a program needn't handle non-finite values.
Results may differ from a plain program's by a relative error of at most 0.009.
Values sent between devices are 32-bit elements; how exact they have to be, the bound alone decides.
No kernel may reach another device: no remote copies, remote signals or barrier semaphores. Data moves between devices by JAX's collectives and lax.ppermute only.
A program may use at most 192 MiB of HBM per device.

v0:
```python
import jax
import jax.numpy as jnp
from jax import lax
from jax.sharding import PartitionSpec as P

NSIZE = 256
ITERS = 2
letters = "abcd"


def normalize(values):
    return values * lax.rsqrt(jnp.mean(values * values, axis=0) + 1e-06)


def equal_counts(indices, position):
    earlier = jnp.float32(0.0)
    same_count = jnp.float32(0.0)
    for other in range(4):
        match_value = (indices[other] == indices[position]).astype(jnp.float32)
        same_count = same_count + match_value
        if other < position:
            earlier = earlier + match_value
    return (earlier, same_count)


def factor_product(indices):
    product = jnp.float32(1.0)
    for other in range(1, 4):
        earlier, unused = equal_counts(indices, other)
        product = product * (1.0 + earlier)
    return product


def contract_axis(tensor, pieces, position):
    others = [other for other in range(4) if other != position]
    leading = others[0]
    paired = (pieces[others[1]][:, None, :] * pieces[others[2]][None, :, :]).astype(jnp.bfloat16)
    kept = "".join(sorted(letters[position] + letters[leading]))
    pattern = "abcd," + letters[others[1]] + letters[others[2]] + "r->" + kept + "r"
    partial_sum = jnp.einsum(pattern, tensor, paired, preferred_element_type=jnp.float32)
    if position < leading:
        return jnp.sum(partial_sum * pieces[leading][None, :, :], axis=1)
    return jnp.sum(partial_sum * pieces[leading][:, None, :], axis=0)


def apply_tensor(tensor_blocks, block_index, current):
    tile_size = tensor_blocks.shape[1]
    blocks_count = NSIZE // tile_size
    total = jnp.zeros(current.shape, jnp.float32)
    for slot_id in range(tensor_blocks.shape[0]):
        tensor = tensor_blocks[slot_id].reshape(tile_size, tile_size, tile_size, tile_size)
        indices = block_index[slot_id]
        live = (indices[0] < blocks_count).astype(jnp.float32)
        safe = jnp.minimum(indices, blocks_count - 1)
        pieces = [
            lax.dynamic_slice_in_dim(current, safe[other] * tile_size, tile_size, 0)
            for other in range(4)
        ]
        weight = live * 6.0 / factor_product(indices)
        for position in range(4):
            result = weight * contract_axis(tensor, pieces, position)
            start = safe[position] * tile_size
            total = lax.dynamic_update_slice_in_dim(
                total, lax.dynamic_slice_in_dim(total, start, tile_size, 0) + result, start, 0
            )
    return total


def body(tensor_blocks, block_index, starts, shifts):
    own_count = starts.shape[1]
    offset = lax.axis_index("blk") * own_count
    own_shifts = lax.dynamic_slice_in_dim(shifts, offset, own_count, 0)
    current_own = normalize(starts)
    current = lax.all_gather(current_own, "blk", axis=1, tiled=True)
    previous_own = current_own
    image_own = current_own
    for step_id in range(ITERS):
        applied = apply_tensor(tensor_blocks, block_index, current)
        final_turn = step_id == ITERS - 1
        summed = lax.psum(applied, "blk")
        image_own = lax.dynamic_slice_in_dim(summed, offset, own_count, 1)
        previous_own = lax.dynamic_slice_in_dim(current, offset, own_count, 1)
        if final_turn:
            current_own = normalize(image_own + own_shifts[None, :] * previous_own)
        else:
            current = normalize(summed + shifts[None, :] * current)
    estimate = jnp.mean(previous_own * image_own, axis=0) * lax.rsqrt(
        jnp.mean(image_own * image_own, axis=0) + 1e-06
    )
    return (current_own, estimate)


def solution(mesh):
    placed = (P("blk", None, None, None), P("blk", None), P(None, "blk"), P())
    return jax.shard_map(
        body, mesh=mesh, in_specs=placed, out_specs=(P(None, "blk"), P("blk")), check_vma=False
    )
```

profile of v0, /device:TPU:0, one launch (start us, length us, event | category | flops | bytes accessed | tf_op | source)
XLA Modules:
  0.0 739.3 jit_solution(965814484213138154)
XLA Ops:
  5.7 43.3 %all-gather = f32[32,1,256]{2,1,0:T(1,128)S(1)} all-gather(f32[1,1,256]{2,1,0:T(1,128)S(1)} %multiply_bitcast_fusion), channel_id=1, replica_groups=mesh['blk'=32] {'blk'}, dimensions={0}, use_global_device_ids=true | all-gather | bytes 33792 | tf_op jit(solution)/shard_map/all_gather | solution.py:74
  63.7 15.7 %fusion.548 = (bf16[1,32,32,1024]{3,2,1,0:T(8,128)(2,1)S(1)}, bf16[1,32,32,1024]{3,2,1,0:T(8,128)(2,1)}, bf16[1,32,32,1024]{3,2,1,0:T(8,128)(2,1)}, bf16[1,32,32...) fusion(bf16[11,32,32,1024]{3,2,1,0:T(8,128)(2,1)} %param.4), kind=kLoop, calls=%fused_computation.877 | loop fusion | bytes 46137344 | tf_op jit(solution)/shard_map/slice | solution.py:51
  79.4 10.9 %reshape_squeeze.44 = bf16[32,32,32,32]{3,2,1,0:T(8,128)(2,1)} reshape(bf16[1,32,32,1024]{3,2,1,0:T(8,128)(2,1)} %get-tuple-element.60) | data formatting | bytes 4194304 | tf_op jit(solution)/shard_map/reshape;squeeze | solution.py:51
  128.8 11.3 %reshape_squeeze.45 = bf16[32,32,32,32]{3,2,1,0:T(8,128)(2,1)} reshape(bf16[1,32,32,1024]{3,2,1,0:T(8,128)(2,1)} %get-tuple-element.59) | data formatting | bytes 4194304 | tf_op jit(solution)/shard_map/reshape;squeeze | solution.py:51
  161.1 11.0 %reshape_squeeze.46 = bf16[32,32,32,32]{3,2,1,0:T(8,128)(2,1)} reshape(bf16[1,32,32,1024]{3,2,1,0:T(8,128)(2,1)} %get-tuple-element.58) | data formatting | bytes 4194304 | tf_op jit(solution)/shard_map/reshape;squeeze | solution.py:51
  192.3 11.1 %reshape_squeeze.47 = bf16[32,32,32,32]{3,2,1,0:T(8,128)(2,1)} reshape(bf16[1,32,32,1024]{3,2,1,0:T(8,128)(2,1)} %get-tuple-element.57) | data formatting | bytes 4194304 | tf_op jit(solution)/shard_map/reshape;squeeze | solution.py:51
  223.7 11.1 %reshape_squeeze.48 = bf16[32,32,32,32]{3,2,1,0:T(8,128)(2,1)} reshape(bf16[1,32,32,1024]{3,2,1,0:T(8,128)(2,1)} %get-tuple-element.56) | data formatting | bytes 4194304 | tf_op jit(solution)/shard_map/reshape;squeeze | solution.py:51
  255.3 11.4 %reshape_squeeze.49 = bf16[32,32,32,32]{3,2,1,0:T(8,128)(2,1)} reshape(bf16[1,32,32,1024]{3,2,1,0:T(8,128)(2,1)} %get-tuple-element.55) | data formatting | bytes 4194304 | tf_op jit(solution)/shard_map/reshape;squeeze | solution.py:51
  287.1 11.0 %reshape_squeeze.50 = bf16[32,32,32,32]{3,2,1,0:T(8,128)(2,1)} reshape(bf16[1,32,32,1024]{3,2,1,0:T(8,128)(2,1)} %get-tuple-element.54) | data formatting | bytes 4194304 | tf_op jit(solution)/shard_map/reshape;squeeze | solution.py:51
  319.5 11.1 %reshape_squeeze.51 = bf16[32,32,32,32]{3,2,1,0:T(8,128)(2,1)} reshape(bf16[1,32,32,1024]{3,2,1,0:T(8,128)(2,1)} %get-tuple-element.53) | data formatting | bytes 4194304 | tf_op jit(solution)/shard_map/reshape;squeeze | solution.py:51
  350.9 11.1 %reshape_squeeze.52 = bf16[32,32,32,32]{3,2,1,0:T(8,128)(2,1)} reshape(bf16[1,32,32,1024]{3,2,1,0:T(8,128)(2,1)} %get-tuple-element.52) | data formatting | bytes 4194304 | tf_op jit(solution)/shard_map/reshape;squeeze | solution.py:51
  382.7 11.3 %reshape_squeeze.53 = bf16[32,32,32,32]{3,2,1,0:T(8,128)(2,1)} reshape(bf16[1,32,32,1024]{3,2,1,0:T(8,128)(2,1)} %get-tuple-element.61) | data formatting | bytes 4194304 | tf_op jit(solution)/shard_map/reshape;squeeze | solution.py:51
  414.6 8.1 %reshape_squeeze.54 = bf16[32,32,32,32]{3,2,1,0:T(8,128)(2,1)} reshape(bf16[1,32,32,1024]{3,2,1,0:T(8,128)(2,1)S(1)} %get-tuple-element.51) | data formatting | bytes 4194304 | tf_op jit(solution)/shard_map/reshape;squeeze | solution.py:51
  443.2 38.1 %psum.14 = f32[256,32]{1,0:T(8,128)S(1)} all-reduce(f32[256,32]{1,0:T(8,128)S(1)} %constant_dynamic-update-slice_fusion.44), channel_id=1, replica_groups=mesh['blk'=32] {'blk'}, use_global_device_ids=true, to_apply=%region_45.0 | all-reduce | flops 8192 | bytes 65536 | tf_op jit(solution)/shard_map/psum | solution.py:80
  493.4 6.9 fusion.174
  512.2 7.3 fusion.172
  531.5 6.9 fusion.170
  550.5 6.9 fusion.168
  569.3 7.1 fusion.166
  607.6 6.9 fusion.162
  626.4 6.9 fusion.160
  664.2 7.1 fusion.156
  683.1 6.9 fusion.154
  690.1 42.2 %psum.15 = f32[256,32]{1,0:T(8,128)S(1)} all-reduce(f32[256,32]{1,0:T(8,128)S(1)} %constant_dynamic-update-slice_fusion), channel_id=1, replica_groups=mesh['blk'=32] {'blk'}, use_global_device_ids=true, to_apply=%region_91.0 | all-reduce | flops 8192 | bytes 65536 | tf_op jit(solution)/shard_map/psum | solution.py:80
  (254 shorter events, 294.9 us)
Async XLA Ops:
  90.3 11.7 %copy-start.11 = (s32[11,4]{0,1:T(4,128)S(1)}, s32[11,4]{0,1:T(4,128)}, u32[]{:S(2)}) copy-start(s32[11,4]{0,1:T(4,128)} %param.5) | copy-start | bytes 532
  95.9 14.8 %copy-start = (bf16[32,32,32,32]{3,2,1,0:T(8,128)(2,1)S(1)}, bf16[32,32,32,32]{3,2,1,0:T(8,128)(2,1)}, u32[]{:S(2)}) copy-start(bf16[32,32,32,32]{3,2,1,0:T(8,128)(2,1)} %reshape_squeeze.44) | copy-start | bytes 6291460
  140.2 14.7 %copy-start.1 = (bf16[32,32,32,32]{3,2,1,0:T(8,128)(2,1)S(1)}, bf16[32,32,32,32]{3,2,1,0:T(8,128)(2,1)}, u32[]{:S(2)}) copy-start(bf16[32,32,32,32]{3,2,1,0:T(8,128)(2,1)} %reshape_squeeze.45) | copy-start | bytes 6291460
  172.2 14.0 %copy-start.2 = (bf16[32,32,32,32]{3,2,1,0:T(8,128)(2,1)S(1)}, bf16[32,32,32,32]{3,2,1,0:T(8,128)(2,1)}, u32[]{:S(2)}) copy-start(bf16[32,32,32,32]{3,2,1,0:T(8,128)(2,1)} %reshape_squeeze.46) | copy-start | bytes 6291460
  203.5 14.1 %copy-start.3 = (bf16[32,32,32,32]{3,2,1,0:T(8,128)(2,1)S(1)}, bf16[32,32,32,32]{3,2,1,0:T(8,128)(2,1)}, u32[]{:S(2)}) copy-start(bf16[32,32,32,32]{3,2,1,0:T(8,128)(2,1)} %reshape_squeeze.47) | copy-start | bytes 6291460
  234.9 14.3 %copy-start.4 = (bf16[32,32,32,32]{3,2,1,0:T(8,128)(2,1)S(1)}, bf16[32,32,32,32]{3,2,1,0:T(8,128)(2,1)}, u32[]{:S(2)}) copy-start(bf16[32,32,32,32]{3,2,1,0:T(8,128)(2,1)} %reshape_squeeze.48) | copy-start | bytes 6291460
  266.8 14.2 %copy-start.5 = (bf16[32,32,32,32]{3,2,1,0:T(8,128)(2,1)S(1)}, bf16[32,32,32,32]{3,2,1,0:T(8,128)(2,1)}, u32[]{:S(2)}) copy-start(bf16[32,32,32,32]{3,2,1,0:T(8,128)(2,1)} %reshape_squeeze.49) | copy-start | bytes 6291460
  298.2 15.1 %copy-start.6 = (bf16[32,32,32,32]{3,2,1,0:T(8,128)(2,1)S(1)}, bf16[32,32,32,32]{3,2,1,0:T(8,128)(2,1)}, u32[]{:S(2)}) copy-start(bf16[32,32,32,32]{3,2,1,0:T(8,128)(2,1)} %reshape_squeeze.50) | copy-start | bytes 6291460
  330.6 14.1 %copy-start.7 = (bf16[32,32,32,32]{3,2,1,0:T(8,128)(2,1)S(1)}, bf16[32,32,32,32]{3,2,1,0:T(8,128)(2,1)}, u32[]{:S(2)}) copy-start(bf16[32,32,32,32]{3,2,1,0:T(8,128)(2,1)} %reshape_squeeze.51) | copy-start | bytes 6291460
  362.1 14.4 %copy-start.8 = (bf16[32,32,32,32]{3,2,1,0:T(8,128)(2,1)S(1)}, bf16[32,32,32,32]{3,2,1,0:T(8,128)(2,1)}, u32[]{:S(2)}) copy-start(bf16[32,32,32,32]{3,2,1,0:T(8,128)(2,1)} %reshape_squeeze.52) | copy-start | bytes 6291460
  394.1 14.4 %copy-start.9 = (bf16[32,32,32,32]{3,2,1,0:T(8,128)(2,1)S(1)}, bf16[32,32,32,32]{3,2,1,0:T(8,128)(2,1)}, u32[]{:S(2)}) copy-start(bf16[32,32,32,32]{3,2,1,0:T(8,128)(2,1)} %reshape_squeeze.53) | copy-start | bytes 6291460
  422.7 14.4 %copy-start.10 = (bf16[32,32,32,32]{3,2,1,0:T(8,128)(2,1)S(1)}, bf16[32,32,32,32]{3,2,1,0:T(8,128)(2,1)}, u32[]{:S(2)}) copy-start(bf16[32,32,32,32]{3,2,1,0:T(8,128)(2,1)} %reshape_squeeze.54) | copy-start | bytes 6291460
  437.2 44.2 %copy-start.12 = (f32[32]{0:T(128)S(1)}, f32[32]{0:T(128)}, u32[]{:S(2)}) copy-start(f32[32]{0:T(128)} %param.7) | copy-start | bytes 388
where the time goes:
time: 754 us; the launch traced here: 739 us
  matrix products  338 us (45%)
  local copies, waits for them, and re-layouts  148 us (20%)
  blocking collectives  124 us (16%)
  between operations  122 us (16%)
    dot_general x66, matrix products, contract_axis(): jnp.einsum(pattern, tensor, paired, preferred_element_type=jnp.float32)  338 us
    another operation x11, local copies, waits for them, and re-layouts, apply_tensor(): tensor_blocks[slot_id].reshape(tile_size, tile_size, tile_size, tile_size)  119 us
    psum x2, blocking collectives, body(): summed = lax.psum(applied, 'blk')  80.3 us
    all_gather x1, blocking collectives, body(): current = lax.all_gather(current_own, 'blk', axis=1, tiled=True)  43.3 us
    slice x1, local copies, waits for them, and re-layouts, apply_tensor(): tensor_blocks[slot_id].reshape(tile_size, tile_size, tile_size, tile_size)  15.7 us

commit v1 on v0

--- a/solution.py
+++ b/solution.py
@@ -6,6 +6,7 @@
 NSIZE = 256
 ITERS = 2
 letters = "abcd"
+pack_slabs = lambda device_axis, x_local: lax.all_gather(x_local, axis_name=device_axis).sum(axis=0)
 
 
 def normalize(values):
@@ -77,7 +78,7 @@
     for step_id in range(ITERS):
         applied = apply_tensor(tensor_blocks, block_index, current)
         final_turn = step_id == ITERS - 1
-        summed = lax.psum(applied, "blk")
+        summed = pack_slabs("blk", applied)
         image_own = lax.dynamic_slice_in_dim(summed, offset, own_count, 1)
         previous_own = lax.dynamic_slice_in_dim(current, offset, own_count, 1)
         if final_turn:

time: 754 us -> 757 us (level)
  waiting for transfers between devices: 0 us -> 102 us
  blocking collectives: 124 us -> 43.3 us
  matrix products: 338 us -> 304 us
  between operations: 122 us -> 137 us
    all_gather x0 -> x2, waiting for transfers between devices: none -> 102 us  [lax.all_gather(x_local, axis_name=device_axis).sum(axis=0)]
    psum x2 -> x0, blocking collectives: 80.3 us -> none  [body(): summed = lax.psum(applied, 'blk')]
    dot_general x66, matrix products: 338 us -> 304 us  [contract_axis(): jnp.einsum(pattern, tensor, paired, preferred_element_type=jnp.float32)]
  transfers between devices with their start and end apart: 0 -> 2, of which waited for: 0 -> 2; matrix products, arithmetic and copies ran while one was open for 0% -> 0% of each run, Pallas kernels for 0% -> 0%
where the time goes in v1:
time: 757 us; the launch traced here: 749 us
  matrix products  304 us (40%)
  local copies, waits for them, and re-layouts  154 us (20%)
  between operations  137 us (18%)
  waiting for transfers between devices  102 us (13%)
  blocking collectives  43.3 us (6%)
  other arithmetic  8.96 us (1%)
    dot_general x66, matrix products, contract_axis(): jnp.einsum(pattern, tensor, paired, preferred_element_type=jnp.float32)  304 us
    another operation x11, local copies, waits for them, and re-layouts, apply_tensor(): tensor_blocks[slot_id].reshape(tile_size, tile_size, tile_size, tile_size)  120 us
    all_gather x2, waiting for transfers between devices, lax.all_gather(x_local, axis_name=device_axis).sum(axis=0)  102 us
    all_gather x1, blocking collectives, body(): current = lax.all_gather(current_own, 'blk', axis=1, tiled=True)  43.3 us
    slice x1, local copies, waits for them, and re-layouts, apply_tensor(): tensor_blocks[slot_id].reshape(tile_size, tile_size, tile_size, tile_size)  16.1 us
  transfers between devices with their start and end apart: 2, of which 2 were waited for; matrix products, arithmetic and copies ran while one was open for 0% of the time, Pallas kernels for 0%

profile of v1, /device:TPU:0, one launch (start us, length us, event | category | flops | bytes accessed | tf_op | source)
XLA Modules:
  0.0 749.5 jit_solution(15829074523614100602)
XLA Ops:
  136.9 43.3 %all-gather = f32[32,1,256]{2,1,0:T(1,128)S(1)} all-gather(f32[1,1,256]{2,1,0:T(1,128)S(1)} %multiply_bitcast_fusion), channel_id=1, replica_groups=mesh['blk'=32] {'blk'}, dimensions={0}, use_global_device_ids=true | all-gather | bytes 33792 | tf_op jit(solution)/shard_map/all_gather | solution.py:75
  182.3 16.1 %fusion.552 = (bf16[1,32,32,1024]{3,2,1,0:T(8,128)(2,1)S(1)}, bf16[1,32,32,1024]{3,2,1,0:T(8,128)(2,1)}, bf16[1,32,32,1024]{3,2,1,0:T(8,128)(2,1)}, bf16[1,32,32...) fusion(bf16[11,32,32,1024]{3,2,1,0:T(8,128)(2,1)} %param.4), kind=kLoop, calls=%fused_computation.882 | loop fusion | bytes 46137344 | tf_op jit(solution)/shard_map/slice | solution.py:52
  198.4 10.9 %reshape_squeeze.45 = bf16[32,32,32,32]{3,2,1,0:T(8,128)(2,1)} reshape(bf16[1,32,32,1024]{3,2,1,0:T(8,128)(2,1)} %get-tuple-element.58) | data formatting | bytes 4194304 | tf_op jit(solution)/shard_map/reshape;squeeze | solution.py:52
  221.4 11.4 %reshape_squeeze.44 = bf16[32,32,32,32]{3,2,1,0:T(8,128)(2,1)} reshape(bf16[1,32,32,1024]{3,2,1,0:T(8,128)(2,1)} %get-tuple-element.59) | data formatting | bytes 4194304 | tf_op jit(solution)/shard_map/reshape;squeeze | solution.py:52
  245.1 11.0 %reshape_squeeze.46 = bf16[32,32,32,32]{3,2,1,0:T(8,128)(2,1)} reshape(bf16[1,32,32,1024]{3,2,1,0:T(8,128)(2,1)} %get-tuple-element.57) | data formatting | bytes 4194304 | tf_op jit(solution)/shard_map/reshape;squeeze | solution.py:52
  268.4 11.1 %reshape_squeeze.47 = bf16[32,32,32,32]{3,2,1,0:T(8,128)(2,1)} reshape(bf16[1,32,32,1024]{3,2,1,0:T(8,128)(2,1)} %get-tuple-element.56) | data formatting | bytes 4194304 | tf_op jit(solution)/shard_map/reshape;squeeze | solution.py:52
  291.8 11.1 %reshape_squeeze.48 = bf16[32,32,32,32]{3,2,1,0:T(8,128)(2,1)} reshape(bf16[1,32,32,1024]{3,2,1,0:T(8,128)(2,1)} %get-tuple-element.55) | data formatting | bytes 4194304 | tf_op jit(solution)/shard_map/reshape;squeeze | solution.py:52
  315.1 11.4 %reshape_squeeze.49 = bf16[32,32,32,32]{3,2,1,0:T(8,128)(2,1)} reshape(bf16[1,32,32,1024]{3,2,1,0:T(8,128)(2,1)} %get-tuple-element.54) | data formatting | bytes 4194304 | tf_op jit(solution)/shard_map/reshape;squeeze | solution.py:52
  338.7 11.0 %reshape_squeeze.50 = bf16[32,32,32,32]{3,2,1,0:T(8,128)(2,1)} reshape(bf16[1,32,32,1024]{3,2,1,0:T(8,128)(2,1)} %get-tuple-element.53) | data formatting | bytes 4194304 | tf_op jit(solution)/shard_map/reshape;squeeze | solution.py:52
  362.0 11.1 %reshape_squeeze.51 = bf16[32,32,32,32]{3,2,1,0:T(8,128)(2,1)} reshape(bf16[1,32,32,1024]{3,2,1,0:T(8,128)(2,1)} %get-tuple-element.52) | data formatting | bytes 4194304 | tf_op jit(solution)/shard_map/reshape;squeeze | solution.py:52
  385.4 11.1 %reshape_squeeze.52 = bf16[32,32,32,32]{3,2,1,0:T(8,128)(2,1)} reshape(bf16[1,32,32,1024]{3,2,1,0:T(8,128)(2,1)} %get-tuple-element.51) | data formatting | bytes 4194304 | tf_op jit(solution)/shard_map/reshape;squeeze | solution.py:52
  408.7 11.3 %reshape_squeeze.53 = bf16[32,32,32,32]{3,2,1,0:T(8,128)(2,1)} reshape(bf16[1,32,32,1024]{3,2,1,0:T(8,128)(2,1)} %get-tuple-element.60) | data formatting | bytes 4194304 | tf_op jit(solution)/shard_map/reshape;squeeze | solution.py:52
  432.3 8.1 %reshape_squeeze.54 = bf16[32,32,32,32]{3,2,1,0:T(8,128)(2,1)} reshape(bf16[1,32,32,1024]{3,2,1,0:T(8,128)(2,1)S(1)} %get-tuple-element.50) | data formatting | bytes 4194304 | tf_op jit(solution)/shard_map/reshape;squeeze | solution.py:52
  454.9 49.6 %all-gather.4.cloned.1.call-done = f32[32,256,32]{1,2,0:T(8,128)} async-done(((f32[1,256,32]{1,2,0:T(8,128)}), f32[32,256,32]{1,2,0:T(8,128)}) %all-gather.4.cloned.1.call-update) | async-done | bytes 1048592 | tf_op jit(solution)/shard_map/all_gather | solution.py:9
  522.6 7.1 fusion.156
  554.6 7.2 fusion.160
  570.5 7.1 fusion.162
  586.5 7.1 fusion.164
  602.3 7.5 fusion.166
  618.5 7.1 fusion.168
  634.2 7.2 fusion.170
  650.1 7.1 fusion.172
  666.2 7.1 fusion.174
  683.9 52.2 %all-gather.6.cloned.1.call-done = f32[32,256,32]{1,2,0:T(8,128)} async-done(((f32[1,256,32]{1,2,0:T(8,128)}), f32[32,256,32]{1,2,0:T(8,128)}) %all-gather.6.cloned.1.call-update) | async-done | bytes 1048592 | tf_op jit(solution)/shard_map/all_gather | solution.py:9
  (330 shorter events, 267.0 us)
Async XLA Ops:
  7.2 497.3 %all-gather.4.cloned.1.call-start = ((), (), s32[]{:S(2)}) async-start(), calls=%async_computation | async-start | bytes 1081344 | tf_op jit(solution)/shard_map/all_gather | solution.py:9
  180.2 18.2 %copy-start.11 = (f32[32,1,256]{2,1,0:T(1,128)}, f32[32,1,256]{2,1,0:T(1,128)S(1)}, u32[]{:S(2)}) copy-start(f32[32,1,256]{2,1,0:T(1,128)S(1)} %all-gather) | copy-start | bytes 98308
  256.2 7.1 copy-start.2
  279.5 7.1 copy-start.3
  302.9 7.1 copy-start.4
  326.5 7.1 copy-start.5
  349.8 7.1 copy-start.6
  373.1 7.1 copy-start.7
  396.5 7.1 copy-start.8
  420.1 7.1 copy-start.9
  449.9 55.9 %copy-start.12 = (f32[32,1,256]{2,1,0:T(1,128)S(1)}, f32[32,1,256]{2,1,0:T(1,128)}, u32[]{:S(2)}) copy-start(f32[32,1,256]{2,1,0:T(1,128)} %copy-done.11) | copy-start | bytes 98308
  449.9 55.9 %copy-start.13 = (f32[32]{0:T(128)S(1)}, f32[32]{0:T(128)}, u32[]{:S(2)}) copy-start(f32[32]{0:T(128)} %param.7) | copy-start | bytes 388
  454.6 281.4 %all-gather.6.cloned.1.call-start = ((), (), s32[]{:S(2)}) async-start(), calls=%async_computation.1 | async-start | bytes 1081344 | tf_op jit(solution)/shard_map/all_gather | solution.py:9
  506.8 13.0 %slice-start.20 = ((s8[8388608]{0:T(1024)(128)(4,1)}), s8[4194304]{0:T(1024)(128)(4,1)S(1)}, s32[]{:S(2)}) async-start(s8[8388608]{0:T(1024)(128)(4,1)} %bitcast.1075), calls=%async_computation.22 | async-start | bytes 8388608
  522.6 13.4 %slice-start.18 = ((s8[8388608]{0:T(1024)(128)(4,1)}), s8[4194304]{0:T(1024)(128)(4,1)S(1)}, s32[]{:S(2)}) async-start(s8[8388608]{0:T(1024)(128)(4,1)} %bitcast.1073), calls=%async_computation.20 | async-start | bytes 8388608
  538.8 13.0 %slice-start.16 = ((s8[8388608]{0:T(1024)(128)(4,1)}), s8[4194304]{0:T(1024)(128)(4,1)S(1)}, s32[]{:S(2)}) async-start(s8[8388608]{0:T(1024)(128)(4,1)} %bitcast.1071), calls=%async_computation.18 | async-start | bytes 8388608
  554.6 13.2 %slice-start.14 = ((s8[8388608]{0:T(1024)(128)(4,1)}), s8[4194304]{0:T(1024)(128)(4,1)S(1)}, s32[]{:S(2)}) async-start(s8[8388608]{0:T(1024)(128)(4,1)} %bitcast.1069), calls=%async_computation.16 | async-start | bytes 8388608
  570.5 13.0 %slice-start.12 = ((s8[8388608]{0:T(1024)(128)(4,1)}), s8[4194304]{0:T(1024)(128)(4,1)S(1)}, s32[]{:S(2)}) async-start(s8[8388608]{0:T(1024)(128)(4,1)} %bitcast.1067), calls=%async_computation.14 | async-start | bytes 8388608
  586.5 13.0 %slice-start.10 = ((s8[8388608]{0:T(1024)(128)(4,1)}), s8[4194304]{0:T(1024)(128)(4,1)S(1)}, s32[]{:S(2)}) async-start(s8[8388608]{0:T(1024)(128)(4,1)} %bitcast.1065), calls=%async_computation.12 | async-start | bytes 8388608
  602.3 13.4 %slice-start.8 = ((s8[8388608]{0:T(1024)(128)(4,1)}), s8[4194304]{0:T(1024)(128)(4,1)S(1)}, s32[]{:S(2)}) async-start(s8[8388608]{0:T(1024)(128)(4,1)} %bitcast.1063), calls=%async_computation.10 | async-start | bytes 8388608
  618.5 13.0 %slice-start.6 = ((s8[8388608]{0:T(1024)(128)(4,1)}), s8[4194304]{0:T(1024)(128)(4,1)S(1)}, s32[]{:S(2)}) async-start(s8[8388608]{0:T(1024)(128)(4,1)} %bitcast.1061), calls=%async_computation.8 | async-start | bytes 8388608
  634.2 13.2 %slice-start.4 = ((s8[8388608]{0:T(1024)(128)(4,1)}), s8[4194304]{0:T(1024)(128)(4,1)S(1)}, s32[]{:S(2)}) async-start(s8[8388608]{0:T(1024)(128)(4,1)} %bitcast.1059), calls=%async_computation.6 | async-start | bytes 8388608
  650.1 13.3 %slice-start.2 = ((s8[8388608]{0:T(1024)(128)(4,1)}), s8[4194304]{0:T(1024)(128)(4,1)S(1)}, s32[]{:S(2)}) async-start(s8[8388608]{0:T(1024)(128)(4,1)} %bitcast.1057), calls=%async_computation.4 | async-start | bytes 8388608
  666.2 13.0 %slice-start = ((s8[8388608]{0:T(1024)(128)(4,1)}), s8[4194304]{0:T(1024)(128)(4,1)S(1)}, s32[]{:S(2)}) async-start(s8[8388608]{0:T(1024)(128)(4,1)} %bitcast.1055), calls=%async_computation.2 | async-start | bytes 8388608
  (14 other events, 87.2 us)
Sparse Core Ops, SparseCore 0:
  454.8 49.6 all-gather.3
  683.5 52.5 all-gather.5
